TPU v7x, 32 devices: a whole 2x2x4 slice. The times are simulated.
32 devices in a mesh: dp: 2 (over x), expert: 16 (over z, y, core).
Axes of the slice: x: 2, y: 2, z: 4, core: 2. Of those that a mesh axis runs over, the one named last changes fastest.
Arguments:
- tokens: bfloat16 [4096, 2048], P(('dp', 'expert')), may hold values from -6 to 6
- grad_out: bfloat16 [4096, 2048], P(('dp', 'expert')), may hold values from -0.125 to 0.125
- router_weight: bfloat16 [2048, 16], replicated, may hold values from -0.125 to 0.125
- expert_index: int32 [4096, 8], P(('dp', 'expert')), may hold values from 0 to 15, all different within a row; in each aligned block of 128 rows (0 to 127, 128 to 255, ...) at most 96 rows name the same one
- w_gate: bfloat16 [16, 2048, 768], P('expert'), may hold values from -0.125 to 0.125
- w_up: bfloat16 [16, 2048, 768], P('expert'), may hold values from -0.125 to 0.125
- w_down: bfloat16 [16, 768, 2048], P('expert'), may hold values from -0.21875 to 0.21875
Outputs:
- gate_grad: float32 [4096, 8], P(('dp', 'expert'))
- router_grad: float32 [2048, 16], P('expert')
Inputs may be any that keep to these rules, and one draw needn't show every extreme that they name: `expert_index`: each row names 8 different experts. In each aligned block of 128 rows (the rows of one device) no expert is named by more than 96 rows, a bound that some blocks reach.
All inputs are finite; a program needn't handle non-finite values.
Results may differ from a plain program's by a relative error of at most 0.009.
Values may be sent and summed in bfloat16 or wider, within the bound.
A program may use at most 128 MiB of HBM per device.

v0:
```python
import jax
import jax.numpy as jnp
from jax import lax
from jax.sharding import PartitionSpec as P


def on_device(tokens, grad_out, router_weight, expert_index, w_gate, w_up, w_down):
    tok_rows, width = tokens.shape
    top = expert_index.shape[1]
    experts = router_weight.shape[1]
    capacity = min(tok_rows, max(2, 3 * tok_rows * top // (2 * experts)))
    slots_all = experts * capacity
    labels = jnp.arange(experts, dtype=jnp.int32)
    hits = (expert_index[:, :, None] == labels).astype(jnp.int32)
    per_token = jnp.sum(hits, axis=1)
    before = jnp.cumsum(per_token, axis=0) - per_token
    slot = jnp.sum(hits * before[:, None, :], axis=2)
    place = expert_index * capacity + slot
    positions = jnp.arange(slots_all, dtype=jnp.int32)
    chosen_map = jnp.any(place[None, :, :] == positions[:, None, None], axis=2).astype(jnp.bfloat16)
    send_rows = jnp.dot(chosen_map, tokens, preferred_element_type=jnp.float32).astype(jnp.bfloat16)
    send_rows = send_rows.reshape(experts, capacity, width)
    gate_w = w_gate[0]
    up_w = w_up[0]
    down_w = w_down[0]
    rows = lax.all_to_all(send_rows, "expert", split_axis=0, concat_axis=0, tiled=True)
    flat = rows.reshape(-1, width)
    gate_in = jnp.dot(flat, gate_w, preferred_element_type=jnp.float32)
    up_in = jnp.dot(flat, up_w, preferred_element_type=jnp.float32)
    hidden = (jax.nn.silu(gate_in) * up_in).astype(jnp.bfloat16)
    produced = (
        jnp.dot(hidden, down_w, preferred_element_type=jnp.float32)
        .astype(jnp.bfloat16)
        .reshape(rows.shape)
    )
    returned = lax.all_to_all(produced, "expert", split_axis=0, concat_axis=0, tiled=True)
    picked = returned.reshape(slots_all, width)[place.reshape(-1)].reshape(tok_rows, top, width)
    gate_grad = lax.dot_general(
        picked, grad_out, (((2,), (1,)), ((0,), (0,))), preferred_element_type=jnp.float32
    )
    logits = jnp.dot(tokens, router_weight, preferred_element_type=jnp.float32)
    masks = hits.astype(jnp.float32)
    chosen = jnp.sum(masks * logits[:, None, :], axis=2)
    weights = jnp.exp(chosen)
    gates = weights / jnp.sum(weights, axis=1, keepdims=True)
    mean_term = jnp.sum(gates * gate_grad, axis=1, keepdims=True)
    logit_grad = gates * (gate_grad - mean_term)
    dense = jnp.sum(logit_grad[:, :, None] * masks, axis=1)
    wide_tokens = tokens.astype(jnp.float32)
    mine = lax.psum_scatter(
        jnp.dot(wide_tokens.T, dense, precision=lax.Precision.HIGHEST),
        "expert",
        scatter_dimension=0,
        tiled=True,
    )
    router_grad = lax.psum(mine, "dp")
    return (gate_grad, router_grad)


def solution(mesh):
    in_specs = (
        P(("dp", "expert"), None),
        P(("dp", "expert"), None),
        P(),
        P(("dp", "expert"), None),
        P("expert", None, None),
        P("expert", None, None),
        P("expert", None, None),
    )
    out_specs = (P(("dp", "expert"), None), P("expert", None))
    return jax.shard_map(
        on_device, mesh=mesh, in_specs=in_specs, out_specs=out_specs, check_vma=False
    )
```

profile of v0, /device:TPU:0, one launch (start us, length us, event | category | flops | bytes accessed | tf_op | source)
XLA Modules:
  0.0 407.9 jit_solution(6692701103044530913)
XLA Ops:
  7.2 0.9 convert_reduce_fusion
  8.0 0.1 copy.18
  8.1 0.2 reduce_window_sum.11
  8.3 0.1 copy.20
  8.4 0.7 select_reduce_fusion
  9.1 0.7 multiply_add_fusion
  9.8 5.6 %fusion = pred[1536,128]{1,0:T(8,128)(4,1)S(1)} fusion(s32[128,8]{0,1:T(8,128)S(1)} %multiply_add_fusion), kind=kLoop, calls=%fused_computation.4 | loop fusion | flops 2949120 | bytes 200704 | tf_op jit(solution)/shard_map/reduce_or | solution.py:20
  15.4 2.8 convolution_convert_fusion.1
  18.2 144.5 %all_to_all.10 = bf16[16,96,2048]{2,1,0:T(8,128)(2,1)S(1)} all-to-all(bf16[16,96,2048]{2,1,0:T(8,128)(2,1)S(1)} %bitcast.32), channel_id=1, replica_groups=mesh['dp'=2,'expert'=16] {'expert'}, dimensions={0} | all-to-all | bytes 12582912 | tf_op jit(solution)/shard_map/all_to_all | solution.py:26
  162.7 5.2 %fusion.5 = f32[1536,768]{1,0:T(8,128)S(1)} fusion(bf16[1536,2048]{1,0:T(8,128)(2,1)S(1)} %bitcast.34, bf16[1,2048,768]{2,1,0:T(8,128)(2,1)S(1)} %copy-done.4), kind=kOutput, calls=%fused_computation.10 | convolution fusion | flops 4831838208 | bytes 14155776 | tf_op jit(solution)/shard_map/dot_general | solution.py:28
  167.9 5.6 %multiply_convert_fusion = bf16[1536,768]{1,0:T(8,128)(2,1)S(1)} fusion(f32[1536,768]{1,0:T(8,128)S(1)} %fusion.5, bf16[1536,2048]{1,0:T(8,128)(2,1)S(1)} %bitcast.35, bf16[1,2048,768]{2,1,0:T(8,128)(2,1)S(1)} %copy-done.5), kind=kOutput, calls=%fused_computation.5 | convolution fusion | flops 4838916096 | bytes 16515072 | tf_op jit(solution)/shard_map/dot_general | solution.py:29
  173.6 7.0 %convolution_convert_fusion = bf16[1536,2048]{1,0:T(8,128)(2,1)} fusion(bf16[1536,768]{1,0:T(8,128)(2,1)S(1)} %multiply_convert_fusion, bf16[1,768,2048]{2,1,0:T(8,128)(2,1)S(1)} %copy-done), kind=kOutput, calls=%fused_computation.1 | convolution fusion | flops 4834983936 | bytes 11796480 | tf_op jit(solution)/shard_map/dot_general | solution.py:32
  180.6 5.7 %all-to-all-start.1 = ((bf16[16,96,2048]{2,1,0:T(8,128)(2,1)}), bf16[16,96,2048]{2,1,0:T(8,128)(2,1)}, u32[]{:S(2)}, u32[]{:S(2)}) async-start(bf16[16,96,2048]{2,1,0:T(8,128)(2,1)} %bitcast.33), calls=%async_computation.1 | async-start | bytes 12582912 | tf_op jit(solution)/shard_map/all_to_all | solution.py:36
  186.3 0.3 reduce-scatter.2.cloned.1.call-start
  186.6 0.1 copy.21
  186.7 0.1 reshape.69
  186.8 1.3 fusion.12
  188.2 112.2 %all-to-all-done.1 = bf16[16,96,2048]{2,1,0:T(8,128)(2,1)} async-done(((bf16[16,96,2048]{2,1,0:T(8,128)(2,1)}), bf16[16,96,2048]{2,1,0:T(8,128)(2,1)}, u32[]{:S(2)}, u32[]{:S(2)}) %all-to-all-start.1) | async-done | bytes 6291488 | tf_op jit(solution)/shard_map/all_to_all | solution.py:36
  300.4 12.4 %gather_fusion = bf16[1024,2048]{1,0:T(8,128)(2,1)} fusion(bf16[1536,2048]{1,0:T(8,128)(2,1)} %bitcast.6, s32[1024]{0:T(1024)S(1)} %broadcast_clamp_fusion), kind=kCustom, calls=%fused_computation | custom fusion | bytes 8392704 | tf_op jit(solution)/shard_map/gather | solution.py:37
  312.8 5.0 %fusion.1 = f32[128,1,8]{2,1,0:T(1,128)S(1)} fusion(bf16[1024,2048]{1,0:T(8,128)(2,1)} %gather_fusion, bf16[128,2048,1]{1,0,2:T(8,128)(2,1)} %bitcast.38), kind=kOutput, calls=%fused_computation.6 | convolution fusion | flops 4194304 | bytes 4722688 | tf_op jit(solution)/shard_map/dot_general | solution.py:38
  317.8 0.1 copy.23
  317.9 2.0 convolution_bitcast_fusion
  319.9 75.4 %reduce-scatter.2.cloned.1.call-done = f32[128,16]{0,1:T(8,128)} async-done(((f32[2048,16]{0,1:T(8,128)}), f32[128,16]{0,1:T(8,128)}) %reduce-scatter.2.cloned.1.call-update) | async-done | bytes 8208 | tf_op jit(solution)/shard_map/reduce_scatter | solution.py:50
  395.3 5.7 %psum.7 = f32[128,16]{0,1:T(8,128)} all-reduce(f32[128,16]{0,1:T(8,128)} %reduce-scatter.2.cloned.1.call-done), channel_id=1, replica_groups=mesh['dp'=2,'expert'=16] {'dp'}, use_global_device_ids=true, to_apply=%region_9.10 | all-reduce | flops 2048 | bytes 16384 | tf_op jit(solution)/shard_map/psum | solution.py:56
  (21 shorter events, 0.2 us)
Async XLA Ops:
  7.2 166.4 %copy-start = (bf16[1,768,2048]{2,1,0:T(8,128)(2,1)S(1)}, bf16[1,768,2048]{2,1,0:T(8,128)(2,1)}, u32[]{:S(2)}) copy-start(bf16[1,768,2048]{2,1,0:T(8,128)(2,1)} %param.13) | copy-start | bytes 9437188
  18.2 144.5 %copy-start.4 = (bf16[1,2048,768]{2,1,0:T(8,128)(2,1)S(1)}, bf16[1,2048,768]{2,1,0:T(8,128)(2,1)}, u32[]{:S(2)}) copy-start(bf16[1,2048,768]{2,1,0:T(8,128)(2,1)} %param.11) | copy-start | bytes 9437188
  162.7 5.2 %copy-start.5 = (bf16[1,2048,768]{2,1,0:T(8,128)(2,1)S(1)}, bf16[1,2048,768]{2,1,0:T(8,128)(2,1)}, u32[]{:S(2)}) copy-start(bf16[1,2048,768]{2,1,0:T(8,128)(2,1)} %param.12) | copy-start | bytes 9437188
  180.6 6.2 %copy-start.2 = (bf16[2048,16]{0,1:T(8,128)(2,1)S(1)}, bf16[2048,16]{0,1:T(8,128)(2,1)}, u32[]{:S(2)}) copy-start(bf16[2048,16]{0,1:T(8,128)(2,1)} %param.9) | copy-start | bytes 196612
  180.6 7.5 %copy-start.1 = (s32[128,8]{0,1:T(8,128)S(1)}, s32[128,8]{0,1:T(8,128)}, u32[]{:S(2)}) copy-start(s32[128,8]{0,1:T(8,128)} %param.10) | copy-start | bytes 12292
  180.6 119.8 %all-to-all-start.1 = ((bf16[16,96,2048]{2,1,0:T(8,128)(2,1)}), bf16[16,96,2048]{2,1,0:T(8,128)(2,1)}, u32[]{:S(2)}, u32[]{:S(2)}) async-start(bf16[16,96,2048]{2,1,0:T(8,128)(2,1)} %bitcast.33), calls=%async_computation.1 | async-start | bytes 12582912 | tf_op jit(solution)/shard_map/all_to_all | solution.py:36
  186.3 209.0 %reduce-scatter.2.cloned.1.call-start = ((), (), s32[]{:S(2)}) async-start(), calls=%async_computation.3 | async-start | bytes 139264 | tf_op jit(solution)/shard_map/reduce_scatter | solution.py:50
  317.8 83.2 %copy-start.3 = (f32[128,1,8]{0,2,1:T(8,128)}, f32[128,1,8]{0,2,1:T(8,128)S(1)}, u32[]{:S(2)}) copy-start(f32[128,1,8]{0,2,1:T(8,128)S(1)} %copy.23) | copy-start | bytes 12292
Sparse Core Ops, SparseCore 0:
  320.1 75.2 reduce-scatter.1
where the time goes:
time: 408 us
  waiting for transfers between devices  188 us (46%)
  blocking collectives  150 us (37%)
  matrix products  28.9 us (7%)
  between operations  14.2 us (3%)
  local copies, waits for them, and re-layouts  12.8 us (3%)
  other arithmetic  8.16 us (2%)
  starting transfers between devices  5.97 us (1%)
    all_to_all x1, blocking collectives, on_device(): lax.all_to_all(send_rows, 'expert', split_axis=0, concat_axis=0, tiled=True)  145 us
    all_to_all x1, waiting for transfers between devices, on_device(): lax.all_to_all(produced, 'expert', split_axis=0, concat_axis=0, tiled=True)  112 us
    reduce_scatter x1, waiting for transfers between devices, on_device(): lax.psum_scatter(jnp.dot(wide_tokens.T, dense, precision=lax.Precision.HI...  75.4 us
    gather x1, local copies, waits for them, and re-layouts, on_device(): returned.reshape(slots_all, width)[place.reshape(-1)]  12.4 us
  transfers between devices with their start and end apart: 2, of which 2 were waited for; matrix products, arithmetic and copies ran while one was open for 0% of the time, Pallas kernels for 0%

commit v1 on v0

v1 whole, which is shorter than its diff:
```python
import jax
import jax.numpy as jnp
from jax import lax
from jax.sharding import PartitionSpec as P


def on_device(tokens, grad_out, router_weight, expert_index, w_gate, w_up, w_down):
    tok_rows, width = tokens.shape
    top = expert_index.shape[1]
    experts = router_weight.shape[1]
    me = lax.axis_index("expert")
    n = lax.axis_size("expert")
    index_all = lax.all_gather(expert_index, "expert", axis=0, tiled=True)
    tok_all = lax.all_gather(tokens, "expert", axis=0, tiled=True)
    grad_all = lax.all_gather(grad_out, "expert", axis=0, tiled=True)
    gate_in = jnp.dot(tok_all, w_gate[0], preferred_element_type=jnp.float32)
    up_in = jnp.dot(tok_all, w_up[0], preferred_element_type=jnp.float32)
    hidden = jax.nn.silu(gate_in) * up_in
    back = lax.dot_general(
        grad_all, w_down[0], (((1,), (1,)), ((), ())), preferred_element_type=jnp.float32
    )
    dots = jnp.sum(hidden * back, axis=1)
    dots_all = lax.all_gather(dots, "expert", axis=0).T
    labels = jnp.arange(experts, dtype=jnp.int32)
    picked = jnp.any(index_all[:, :, None] == labels, axis=1)
    logits = jnp.dot(tok_all, router_weight, preferred_element_type=jnp.float32)
    weights = jnp.where(picked, jnp.exp(jnp.where(picked, logits, 0.0)), 0.0)
    gates = weights / jnp.sum(weights, axis=1, keepdims=True)
    kept = jnp.where(picked, dots_all, 0.0)
    dense = gates * (kept - jnp.sum(gates * kept, axis=1, keepdims=True))
    cols = width // n
    mine = lax.dynamic_slice_in_dim(tok_all, me * cols, cols, axis=1)
    high = dense.astype(jnp.bfloat16)
    low = (dense - high.astype(jnp.float32)).astype(jnp.bfloat16)
    both = jnp.concatenate([high, low], axis=1)
    part = lax.dot_general(
        mine, both, (((0,), (0,)), ((), ())), preferred_element_type=jnp.float32
    )
    router_grad = lax.psum(part[:, :experts] + part[:, experts:], "dp")
    own = lax.dynamic_slice_in_dim(dots_all, me * tok_rows, tok_rows, axis=0)
    hits = (expert_index[:, :, None] == labels).astype(jnp.float32)
    gate_grad = jnp.sum(hits * own[:, None, :], axis=2)
    return (gate_grad, router_grad)


def solution(mesh):
    in_specs = (
        P(("dp", "expert"), None),
        P(("dp", "expert"), None),
        P(),
        P(("dp", "expert"), None),
        P("expert", None, None),
        P("expert", None, None),
        P("expert", None, None),
    )
    out_specs = (P(("dp", "expert"), None), P("expert", None))
    return jax.shard_map(
        on_device, mesh=mesh, in_specs=in_specs, out_specs=out_specs, check_vma=False
    )
```

time: 408 us -> 216 us (0.53)
  blocking collectives: 150 us -> 48.9 us
  waiting for transfers between devices: 188 us -> 110 us
  local copies, waits for them, and re-layouts: 12.8 us -> 0.07 us
  matrix products: 28.9 us -> 41.4 us
  other arithmetic: 8.16 us -> 0.84 us
  starting transfers between devices: 5.97 us -> 0.08 us
    all_to_all x1 -> x0, blocking collectives: 145 us -> none  [on_device(): lax.all_to_all(send_rows, 'expert', split_axis=0, concat_axis=0, tiled=True)]
    all_to_all x1 -> x0, waiting for transfers between devices: 112 us -> none  [on_device(): lax.all_to_all(produced, 'expert', split_axis=0, concat_axis=0, tiled=True)]
    all_gather x0 -> x2, waiting for transfers between devices: none -> 109 us  [the longest x1 54.5 us: on_device(): grad_all = lax.all_gather(grad_out, 'expert', axis=0, tiled=True)]
    reduce_scatter x1 -> x0, waiting for transfers between devices: 75.4 us -> none  [on_device(): lax.psum_scatter(jnp.dot(wide_tokens.T, dense, precision=lax.Precision.HI...]
    all_gather x0 -> x2, blocking collectives: none -> 43.3 us  [the longest x1 24 us: on_device(): index_all = lax.all_gather(expert_index, 'expert', axis=0, tiled=True)]
    dot_general x7 -> x5, matrix products: 28.9 us -> 41.4 us  [the longest x1 13.9 us: on_device(): lax.dot_general(grad_all, w_down[0], (((1,), (1,)), ((), ())), preferred_...]
    gather x1 -> x0, local copies, waits for them, and re-layouts: 12.4 us -> none  [on_device(): returned.reshape(slots_all, width)[place.reshape(-1)]]
    all_to_all x1 -> x0, starting transfers between devices: 5.7 us -> none  [on_device(): lax.all_to_all(produced, 'expert', split_axis=0, concat_axis=0, tiled=True)]
  transfers between devices with their start and end apart: 2 -> 2, of which waited for: 2 -> 2; matrix products, arithmetic and copies ran while one was open for 0% -> 10% of each run, Pallas kernels for 0% -> 0%
where the time goes in v1:
time: 216 us
  waiting for transfers between devices  110 us (51%)
  blocking collectives  48.9 us (23%)
  matrix products  41.4 us (19%)
  between operations  14.1 us (7%)
    all_gather x1, waiting for transfers between devices, on_device(): grad_all = lax.all_gather(grad_out, 'expert', axis=0, tiled=True)  54.5 us
    all_gather x1, waiting for transfers between devices, on_device(): tok_all = lax.all_gather(tokens, 'expert', axis=0, tiled=True)  54.5 us
    all_gather x1, blocking collectives, on_device(): index_all = lax.all_gather(expert_index, 'expert', axis=0, tiled=True)  24 us
    all_gather x1, blocking collectives, on_device(): dots_all = lax.all_gather(dots, 'expert', axis=0).T  19.3 us
    dot_general x1, matrix products, on_device(): lax.dot_general(grad_all, w_down[0], (((1,), (1,)), ((), ())), preferred_...  13.9 us
    dot_general x1, matrix products, on_device(): up_in = jnp.dot(tok_all, w_up[0], preferred_element_type=jnp.float32)  11.6 us
    dot_general x1, matrix products, on_device(): gate_in = jnp.dot(tok_all, w_gate[0], preferred_element_type=jnp.float32)  8.96 us
    dot_general x1, matrix products, on_device(): logits = jnp.dot(tok_all, router_weight, preferred_element_type=jnp.float32)  5.68 us
  transfers between devices with their start and end apart: 2, of which 2 were waited for; matrix products, arithmetic and copies ran while one was open for 10% of the time, Pallas kernels for 0%

profile of v1, /device:TPU:0, one launch (start us, length us, event | category | flops | bytes accessed | tf_op | source)
XLA Modules:
  0.0 215.8 jit_solution(3040273428123021212)
XLA Ops:
  7.2 0.0 copy-start
  7.2 0.0 all-gather.4.cloned.1.call-start
  7.2 0.7 all-gather.4.cloned.1.call-update
  7.9 0.0 all-gather.6.cloned.1.call-start
  8.0 0.7 all-gather.6.cloned.1.call-update
  8.7 24.0 %all_gather.19 = s32[2048,8]{0,1:T(8,128)S(1)} all-gather(s32[128,8]{0,1:T(8,128)} %param.10), channel_id=1, replica_groups=mesh['dp'=2,'expert'=16] {'expert'}, dimensions={0}, use_global_device_ids=true | all-gather | bytes 69632 | tf_op jit(solution)/shard_map/all_gather | solution.py:13
  32.6 0.1 fusion.7
  32.8 54.5 %all-gather.4.cloned.1.call-done = bf16[2048,2048]{1,0:T(8,128)(2,1)} async-done(((bf16[128,2048]{1,0:T(8,128)(2,1)}), bf16[2048,2048]{1,0:T(8,128)(2,1)}) %all-gather.4.cloned.1.call-update) | async-done | bytes 8388624 | tf_op jit(solution)/shard_map/all_gather | solution.py:14
  87.3 0.0 copy-done
  87.3 11.6 %fusion.1 = f32[2048,768]{0,1:T(8,128)} fusion(bf16[2048,2048]{1,0:T(8,128)(2,1)} %all-gather.4.cloned.1.call-done, bf16[1,2048,768]{2,1,0:T(8,128)(2,1)S(1)} %copy-done), kind=kOutput, calls=%fused_computation.2 | convolution fusion | flops 6442450944 | bytes 17825792 | tf_op jit(solution)/shard_map/dot_general | solution.py:17
  98.9 0.0 copy-done.1
  98.9 0.0 copy-done.4
  98.9 9.0 %fusion.3 = f32[2048,768]{0,1:T(8,128)} fusion(bf16[2048,2048]{1,0:T(8,128)(2,1)S(1)} %copy-done.1, bf16[1,2048,768]{2,1,0:T(8,128)(2,1)S(1)} %copy-done.4), kind=kOutput, calls=%fused_computation.4 | convolution fusion | flops 6442450944 | bytes 17825792 | tf_op jit(solution)/shard_map/dot_general | solution.py:16
  107.8 54.5 %all-gather.6.cloned.1.call-done = bf16[2048,2048]{1,0:T(8,128)(2,1)} async-done(((bf16[128,2048]{1,0:T(8,128)(2,1)}), bf16[2048,2048]{1,0:T(8,128)(2,1)}) %all-gather.6.cloned.1.call-update) | async-done | bytes 8388624 | tf_op jit(solution)/shard_map/all_gather | solution.py:15
  162.4 13.9 %multiply_reduce_fusion = f32[2048]{0:T(1024)S(1)} fusion(f32[2048,768]{0,1:T(8,128)} %fusion.1, f32[2048,768]{0,1:T(8,128)} %fusion.3, bf16[2048,2048]{1,0:T(8,128)(2,1)} %all-gather.6.cloned.1.call-done, bf16[1,768,2048]{2,1,0:T(8,128)(2,1)} %param.13), kind=kOutput, calls=%fused_computation | convolution fusion | flops 6453458944 | bytes 24125440 | tf_op jit(solution)/shard_map/dot_general | solution.py:19
  176.3 19.3 %all-gather = f32[32768]{0:T(1024)S(1)} all-gather(f32[2048]{0:T(1024)S(1)} %multiply_reduce_fusion), channel_id=2, replica_groups=mesh['dp'=2,'expert'=16] {'expert'}, dimensions={0}, use_global_device_ids=true | all-gather | bytes 139264 | tf_op jit(solution)/shard_map/all_gather | solution.py:23
  195.7 0.0 copy-done.2
  195.7 0.0 copy-start.3
  195.7 5.7 %fusion.16 = (f32[2048]{0:T(1024)S(1)}, f32[2048,16]{0,1:T(8,128)S(1)}) fusion(pred[2048,16]{0,1:T(8,128)(4,1)S(1)} %fusion.7, bf16[2048,2048]{1,0:T(8,128)(2,1)} %all-gather.4.cloned.1.call-done, bf16[2048,16]{0,1:T(8,128)(2,1)S(1)} %copy-done.2), kind=kOutput, calls=%fused_computation.28 | convolution fusion | flops 134313984 | bytes 8626176 | tf_op jit(solution)/shard_map/dot_general | solution.py:26
  201.4 0.1 multiply_reduce_fusion.1
  201.4 0.1 fusion.15
  201.5 1.2 fusion.8
  202.8 5.6 %psum.7 = f32[128,16]{0,1:T(8,128)} all-reduce(f32[128,16]{0,1:T(8,128)S(1)} %slice_add_fusion), channel_id=1, replica_groups=mesh['dp'=2,'expert'=16] {'dp'}, use_global_device_ids=true, to_apply=%region_5.6 | all-reduce | flops 2048 | bytes 16384 | tf_op jit(solution)/shard_map/psum | solution.py:39
  208.4 0.6 select_reduce_fusion
  (7 shorter events, 0.1 us)
Async XLA Ops:
  7.2 80.1 %copy-start = (bf16[1,2048,768]{2,1,0:T(8,128)(2,1)S(1)}, bf16[1,2048,768]{2,1,0:T(8,128)(2,1)}, u32[]{:S(2)}) copy-start(bf16[1,2048,768]{2,1,0:T(8,128)(2,1)} %param.12) | copy-start | bytes 9437188
  7.2 80.1 %all-gather.4.cloned.1.call-start = ((), (), s32[]{:S(2)}) async-start(), calls=%async_computation | async-start | bytes 8912896 | tf_op jit(solution)/shard_map/all_gather | solution.py:14
  7.9 154.4 %all-gather.6.cloned.1.call-start = ((), (), s32[]{:S(2)}) async-start(), calls=%async_computation.1 | async-start | bytes 8912896 | tf_op jit(solution)/shard_map/all_gather | solution.py:15
  87.3 11.6 %copy-start.1 = (bf16[2048,2048]{1,0:T(8,128)(2,1)S(1)}, bf16[2048,2048]{1,0:T(8,128)(2,1)}, u32[]{:S(2)}) copy-start(bf16[2048,2048]{1,0:T(8,128)(2,1)} %all-gather.4.cloned.1.call-done) | copy-start | bytes 25165828
  87.3 11.6 %copy-start.4 = (bf16[1,2048,768]{2,1,0:T(8,128)(2,1)S(1)}, bf16[1,2048,768]{2,1,0:T(8,128)(2,1)}, u32[]{:S(2)}) copy-start(bf16[1,2048,768]{2,1,0:T(8,128)(2,1)} %param.11) | copy-start | bytes 9437188
  107.8 87.9 %copy-start.2 = (bf16[2048,16]{0,1:T(8,128)(2,1)S(1)}, bf16[2048,16]{0,1:T(8,128)(2,1)}, u32[]{:S(2)}) copy-start(bf16[2048,16]{0,1:T(8,128)(2,1)} %param.9) | copy-start | bytes 196612
  195.7 12.7 %copy-start.3 = (s32[128,8]{0,1:T(8,128)S(1)}, s32[128,8]{0,1:T(8,128)}, u32[]{:S(2)}) copy-start(s32[128,8]{0,1:T(8,128)} %param.10) | copy-start | bytes 12292
Sparse Core Ops, SparseCore 0:
  10.2 77.0 all-gather.3
  89.5 72.8 all-gather.5

commit v2 on v1

--- a/solution.py
+++ b/solution.py
@@ -1,10 +1,14 @@
+import functools
+
 import jax
 import jax.numpy as jnp
 from jax import lax
+from jax.experimental import pallas as pl
+from jax.experimental.pallas import tpu as pltpu
 from jax.sharding import PartitionSpec as P
 
 
-def on_device(tokens, grad_out, router_weight, expert_index, w_gate, w_up, w_down):
+def plain(tokens, grad_out, router_weight, expert_index, w_gate, w_up, w_down):
     tok_rows, width = tokens.shape
     top = expert_index.shape[1]
     experts = router_weight.shape[1]
@@ -43,7 +47,321 @@
     return (gate_grad, router_grad)
 
 
+def layer_kernel(n, dp, tok_in, grad_in, rw_in, idx_in, wg_in, wu_in, wd_in, gg_out, rg_out,
+                 tok, grad, idx, wg, wu, wd, hid, eo, lg, dots, part,
+                 s_t, r_t, s_a, r_a, s_c, r_c, s_i, r_i, s_d, r_d, s_w, r_w, s_p, r_p, loc):
+    plane = n // 2
+    line = plane // 2
+    me = lax.axis_index("expert")
+    xd = lax.axis_index("dp")
+    c = me % 2
+    q = me // 2
+    y = q % 2
+    z = q // 2
+    rows, width = tok_in.shape
+    ff = wg_in.shape[2]
+    experts, top = rw_in.shape[0], idx_in.shape[0]
+    cut = rows * 5 // 8
+    pair = 2 * rows
+
+    def dev(zz, yy, cc):
+        return {"expert": (zz * 2 + yy) * 2 + cc}
+
+    def remote(src, dst, ss, rs, where):
+        return pltpu.make_async_remote_copy(
+            src_ref=src, dst_ref=dst, send_sem=ss, recv_sem=rs,
+            device_id=where, device_id_type=pl.DeviceIdType.MESH)
+
+    DOWN, UP, SIDE = 0, 1, 2
+
+    def target(way):
+        if way == DOWN:
+            return dev(z - 1, y, c)
+        if way == UP:
+            return dev(z + 1, y, c)
+        return dev(z, 1 - y, c)
+
+    kinds = {"t": (tok, tok_in, 0, rows, s_t, r_t),
+             "a": (grad, grad_in, 0, cut, s_a, r_a),
+             "c": (grad, grad_in, cut, rows - cut, s_c, r_c)}
+
+    def piece(kind, zb, yb, way, own=False):
+        buf, inp, lo, size, ss, rs = kinds[kind]
+        at = buf.at[zb, pl.ds(pl.multiple_of(yb * rows + lo, 16), size)]
+        src = inp.at[pl.ds(lo, size)] if own else at
+        return remote(src, at, ss.at[zb * 2 + yb, way], rs.at[zb * 2 + yb], target(way))
+
+    def arrived(kind, zb, yb):
+        piece(kind, zb, yb, SIDE).wait_recv()
+
+    barrier = pltpu.get_barrier_semaphore()
+
+    def plane_dev(k):
+        return {"expert": ((q + k) % plane) * 2 + c}
+
+    def owner_dev(k):
+        return {"dp": (xd + k // 2) % dp, "expert": q * 2 + (c + k) % 2}
+
+    for k in range(1, plane):
+        pl.semaphore_signal(barrier, inc=1, device_id=plane_dev(k), device_id_type=pl.DeviceIdType.MESH)
+    for k in range(1, 2 * dp):
+        pl.semaphore_signal(barrier, inc=1, device_id=owner_dev(k), device_id_type=pl.DeviceIdType.MESH)
+    mine = pl.ds(pl.multiple_of(y * rows, 16), rows)
+    local = [pltpu.make_async_copy(tok_in, tok.at[z, mine], loc.at[0]),
+             pltpu.make_async_copy(grad_in, grad.at[z, mine], loc.at[1]),
+             pltpu.make_async_copy(idx_in, idx.at[q], loc.at[2]),
+             pltpu.make_async_copy(wg_in.at[0], wg.at[c], loc.at[3]),
+             pltpu.make_async_copy(wu_in.at[0], wu.at[c], loc.at[4]),
+             pltpu.make_async_copy(wd_in.at[0], wd.at[c], loc.at[5])]
+    for copy in local:
+        copy.start()
+    pl.semaphore_wait(barrier, plane - 1 + 2 * dp - 1)
+
+    def own_z(kind, way):
+        piece(kind, z, y, way, own=True).start()
+
+    pl.when(z > 0)(lambda: own_z("t", DOWN))
+    pl.when(z < line - 1)(lambda: own_z("t", UP))
+    own_z("t", SIDE)
+    other = {"expert": q * 2 + (1 - c)}
+    weights = [remote(wg_in.at[0], wg.at[c], s_w.at[0], r_w.at[0], other),
+               remote(wu_in.at[0], wu.at[c], s_w.at[1], r_w.at[1], other),
+               remote(wd_in.at[0], wd.at[c], s_w.at[2], r_w.at[2], other)]
+    for w in weights:
+        w.start()
+    index_sends = [remote(idx_in, idx.at[q], s_i.at[k], r_i.at[k], plane_dev(k)) for k in range(1, plane)]
+    for w in index_sends:
+        w.start()
+    pl.when(z == 0)(lambda: own_z("a", UP))
+    pl.when(z == line - 1)(lambda: own_z("a", DOWN))
+
+    def relay(kind, s):
+        @pl.when(z + s < line)
+        def _():
+            arrived(kind, z + s, y)
+
+            @pl.when(z > 0)
+            def _():
+                piece(kind, z + s, y, DOWN).start()
+            piece(kind, z + s, y, SIDE).start()
+
+        @pl.when(z - s >= 0)
+        def _():
+            arrived(kind, z - s, y)
+
+            @pl.when(z < line - 1)
+            def _():
+                piece(kind, z - s, y, UP).start()
+            piece(kind, z - s, y, SIDE).start()
+
+    ft = ff // 3 if ff % 384 == 0 else ff
+    dt = width // 4 if width % 512 == 0 else width
+
+    def produce(zp):
+        @pl.loop(0, 2)
+        def _(r):
+            @pl.loop(0, ff // ft)
+            def _(j):
+                at = pl.ds(pl.multiple_of(j * ft, 128), ft)
+                x = tok[zp]
+                g = jnp.dot(x, wg[r, :, at], preferred_element_type=jnp.float32)
+                u = jnp.dot(x, wu[r, :, at], preferred_element_type=jnp.float32)
+                hid[:, at] = (g / (1.0 + jnp.exp(-g)) * u).astype(jnp.bfloat16)
+
+            @pl.loop(0, width // dt)
+            def _(j):
+                at = pl.ds(pl.multiple_of(j * dt, 128), dt)
+                eo[zp, r, :, at] = jnp.dot(
+                    hid[...], wd[r, :, at], preferred_element_type=jnp.float32).astype(jnp.bfloat16)
+        lg[:, pl.ds(pl.multiple_of(zp * pair, 128), pair)] = lax.dot_general(
+            rw_in[...], tok[zp], (((1,), (1,)), ((), ())), preferred_element_type=jnp.float32)
+
+    def produce_ring(s):
+        if s == 0:
+            arrived("t", z, 1 - y)
+            produce(z)
+            return
+
+        @pl.when(z + s < line)
+        def _():
+            arrived("t", z + s, 1 - y)
+            produce(z + s)
+
+        @pl.when(z - s >= 0)
+        def _():
+            arrived("t", z - s, 1 - y)
+            produce(z - s)
+
+    for s in range(1, line):
+        relay("t", s)
+        pl.when(z == s)(lambda: own_z("a", UP)) if s < line - 1 else None
+        pl.when(line - 1 - z == s)(lambda: own_z("a", DOWN)) if s < line - 1 else None
+        if s == line - 1:
+            own_z("c", SIDE)
+            own_z("a", SIDE)
+        if s == 1:
+            for copy in local:
+                copy.wait()
+            for w in weights:
+                w.wait_recv()
+        produce_ring(s - 1)
+
+    for s in range(1, line):
+        relay("a", s)
+        if s == 1:
+            produce_ring(line - 1)
+
+    arrived("c", z, 1 - y)
+    for yb in range(2):
+        pl.when(z > 0)(lambda yb=yb: piece("c", z, yb, DOWN).start())
+        pl.when(z < line - 1)(lambda yb=yb: piece("c", z, yb, UP).start())
+
+    def reduce_pair(zp):
+        @pl.loop(0, 2)
+        def _(r):
+            total = jnp.zeros((pair, 128), jnp.float32)
+            for j in range(width // 128):
+                at = pl.ds(j * 128, 128)
+                total += eo[zp, r, :, at].astype(jnp.float32) * grad[zp, :, at].astype(jnp.float32)
+            row = jnp.sum(total.T, axis=0, keepdims=True)
+            dots[q, pl.ds(r, 1), pl.ds(pl.multiple_of(zp * pair, 128), pair)] = row
+
+    arrived("a", z, 1 - y)
+    reduce_pair(z)
+    for s in range(1, line):
+        def take(zb, way, ok):
+            for yb in range(2):
+                arrived("c", zb, yb)
+                pl.when(ok)(lambda yb=yb: piece("c", zb, yb, way).start())
+
+        pl.when(z + s < line)(lambda: take(z + s, DOWN, z > 0))
+        pl.when(z - s >= 0)(lambda: take(z - s, UP, z < line - 1))
+
+        @pl.when(z + s < line)
+        def _():
+            arrived("a", z + s, 1 - y)
+            reduce_pair(z + s)
+
+        @pl.when(z - s >= 0)
+        def _():
+            arrived("a", z - s, 1 - y)
+            reduce_pair(z - s)
+
+    dot_sends = [remote(dots.at[q], dots.at[q], s_d.at[k], r_d.at[k], plane_dev(k)) for k in range(1, plane)]
+    for w in dot_sends:
+        w.start()
+    for w in index_sends:
+        w.wait()
+    labels = lax.broadcasted_iota(jnp.int32, (experts, plane * rows), 0)
+    chosen = jnp.zeros((experts, plane * rows), jnp.float32)
+    for k in range(top):
+        named = jnp.concatenate([idx[b, pl.ds(k, 1), :] for b in range(plane)], axis=1)
+        chosen = jnp.where(labels == named, 1.0, chosen)
+    weight = jnp.where(chosen > 0.0, jnp.exp(jnp.where(chosen > 0.0, lg[...], 0.0)), 0.0)
+    gates = weight / jnp.sum(weight, axis=0, keepdims=True)
+    for w in dot_sends:
+        w.wait()
+    all_dots = jnp.concatenate([dots[b] for b in range(plane)], axis=0)
+    kept = jnp.where(chosen > 0.0, all_dots, 0.0)
+    dense = gates * (kept - jnp.sum(gates * kept, axis=0, keepdims=True))
+    high = dense.astype(jnp.bfloat16)
+    low = (dense - high.astype(jnp.float32)).astype(jnp.bfloat16)
+    cols = width // n
+    at = pl.ds(pl.multiple_of(q * 2 * cols, 128), 2 * cols)
+    both = jnp.concatenate([high, low], axis=0)
+    split = jnp.zeros((2 * experts, 2 * cols), jnp.float32)
+    for b in range(line):
+        split += jnp.dot(both[:, b * pair:(b + 1) * pair], tok[b, :, at], preferred_element_type=jnp.float32)
+    terms = split[:experts] + split[experts:]
+    part[0, 0] = terms[:, :cols]
+    part[0, 1] = terms[:, cols:]
+    part_sends = [remote(part.at[0, (c + k) % 2], part.at[k, 0], s_p.at[k], r_p.at[k], owner_dev(k))
+                  for k in range(1, 2 * dp)]
+    for w in part_sends:
+        w.start()
+    own = jnp.concatenate(
+        [dots[b, :, pl.ds(pl.multiple_of(q * rows, 128), rows)] for b in range(plane)], axis=0)
+    names = idx[q]
+    small = lax.broadcasted_iota(jnp.int32, (experts, rows), 0)
+    for k in range(top):
+        gg_out[pl.ds(k, 1), :] = jnp.sum(
+            jnp.where(small == names[k:k + 1, :], own, 0.0), axis=0, keepdims=True)
+    for w in part_sends:
+        w.wait()
+    total = part[0, c]
+    for k in range(1, 2 * dp):
+        total += part[k, 0]
+    rg_out[...] = total
+
+    for w in weights:
+        w.wait_send()
+
+    def gone(kind, zb, yb, way):
+        piece(kind, zb, yb, way).wait_send()
+
+    for kind in ("t", "a"):
+        for zb in range(line):
+            pl.when((zb >= z) & (z > 0))(lambda: gone(kind, zb, y, DOWN))
+            pl.when((zb <= z) & (z < line - 1))(lambda: gone(kind, zb, y, UP))
+            gone(kind, zb, y, SIDE)
+    gone("c", z, y, SIDE)
+    for zb in range(line):
+        for yb in range(2):
+            pl.when((zb >= z) & (z > 0))(lambda: gone("c", zb, yb, DOWN))
+            pl.when((zb <= z) & (z < line - 1))(lambda: gone("c", zb, yb, UP))
+
+
+def fused(n, dp, tokens, grad_out, router_weight, expert_index, w_gate, w_up, w_down):
+    rows, width = tokens.shape
+    ff = w_gate.shape[2]
+    top = expert_index.shape[1]
+    experts = router_weight.shape[1]
+    plane, cols = n // 2, width // n
+    line = plane // 2
+    pair = 2 * rows
+    anywhere = pl.BlockSpec(memory_space=pl.ANY)
+    vmem = pl.BlockSpec(memory_space=pltpu.VMEM)
+    dma = pltpu.SemaphoreType.DMA
+    bf, f32 = jnp.bfloat16, jnp.float32
+    gg, rg = pl.pallas_call(
+        functools.partial(layer_kernel, n, dp),
+        out_shape=(jax.ShapeDtypeStruct((top, rows), f32), jax.ShapeDtypeStruct((experts, cols), f32)),
+        in_specs=[anywhere, anywhere, vmem, vmem, anywhere, anywhere, anywhere],
+        out_specs=(vmem, vmem),
+        scratch_shapes=[
+            pltpu.VMEM((line, pair, width), bf),
+            pltpu.VMEM((line, pair, width), bf),
+            pltpu.VMEM((plane, top, rows), jnp.int32),
+            pltpu.VMEM((2, width, ff), bf),
+            pltpu.VMEM((2, width, ff), bf),
+            pltpu.VMEM((2, ff, width), bf),
+            pltpu.VMEM((pair, ff), bf),
+            pltpu.VMEM((line, 2, pair, width), bf),
+            pltpu.VMEM((experts, plane * rows), f32),
+            pltpu.VMEM((plane, 2, plane * rows), f32),
+            pltpu.VMEM((2 * dp, 2, experts, cols), f32),
+            dma((plane, 3)), dma((plane,)), dma((plane, 3)), dma((plane,)), dma((plane, 3)), dma((plane,)),
+            dma((plane,)), dma((plane,)), dma((plane,)), dma((plane,)),
+            dma((3,)), dma((3,)), dma((2 * dp,)), dma((2 * dp,)), dma((6,)),
+        ],
+        compiler_params=pltpu.CompilerParams(
+            collective_id=0, has_side_effects=True, vmem_limit_bytes=60 * 2**20),
+    )(tokens, grad_out, router_weight.T, expert_index.T, w_gate, w_up, w_down)
+    return gg.T, rg.T
+
+
 def solution(mesh):
+    n, dp = mesh.shape["expert"], mesh.shape["dp"]
+
+    def on_device(tokens, grad_out, router_weight, expert_index, w_gate, w_up, w_down):
+        rows, width = tokens.shape
+        ff = w_gate.shape[2]
+        held = 2 * (2 * n // 2 * rows * width * 2 + 6 * ff * width)
+        fits = n % 4 == 0 and n >= 8 and held < 44 * 2**20 and width % (128 * n) == 0
+        fits = fits and rows % 128 == 0 and router_weight.shape[1] == n
+        body = functools.partial(fused, n, dp) if fits else plain
+        return body(tokens, grad_out, router_weight, expert_index, w_gate, w_up, w_down)
+
     in_specs = (
         P(("dp", "expert"), None),
         P(("dp", "expert"), None),

time: 216 us -> 116 us (0.54)
  Pallas kernels: 0 us -> 112 us
  waiting for transfers between devices: 110 us -> 0 us
  blocking collectives: 48.9 us -> 0 us
  matrix products: 41.4 us -> 0 us
  between operations: 14.1 us -> 0.64 us
  local copies, waits for them, and re-layouts: 0.07 us -> 2.56 us
    pallas_call x0 -> x1, Pallas kernels: none -> 112 us  [fused(): pl.pallas_call(functools.partial(layer_kernel, n, dp), out_shape=(jax.Sha...]
    all_gather x2 -> x0, waiting for transfers between devices: 109 us -> none  [the longest x1 54.5 us: on_device(): grad_all = lax.all_gather(grad_out, 'expert', axis=0, tiled=True)]
    all_gather x2 -> x0, blocking collectives: 43.3 us -> none  [the longest x1 24 us: on_device(): index_all = lax.all_gather(expert_index, 'expert', axis=0, tiled=True)]
    dot_general x5 -> x0, matrix products: 41.4 us -> none  [the longest x1 13.9 us: on_device(): lax.dot_general(grad_all, w_down[0], (((1,), (1,)), ((), ())), preferred_...]
    psum x1 -> x0, blocking collectives: 5.59 us -> none  [on_device(): router_grad = lax.psum(part[:, :experts] + part[:, experts:], 'dp')]
    unnamed x10 -> x2, local copies, waits for them, and re-layouts: 0.03 us -> 2.56 us
  transfers between devices with their start and end apart: 2 -> 0, of which waited for: 2 -> 0; matrix products, arithmetic and copies ran while one was open for 10% -> 0% of each run, Pallas kernels for 0% -> 0%
where the time goes in v2:
time: 116 us
  Pallas kernels  112 us (97%)
  local copies, waits for them, and re-layouts  2.56 us (2%)
    pallas_call x1, Pallas kernels, fused(): pl.pallas_call(functools.partial(layer_kernel, n, dp), out_shape=(jax.Sha...  112 us
    unnamed x2, local copies, waits for them, and re-layouts  2.56 us

profile of v2, /device:TPU:0, one launch (start us, length us, event | category | flops | bytes accessed | tf_op | source)
XLA Modules:
  0.0 115.6 jit_solution(1116232630037262416)
XLA Ops:
  0.6 112.4 %shard_map.86 = (f32[8,128]{1,0:T(8,128)}, f32[16,128]{1,0:T(8,128)}) custom-call(bf16[128,2048]{1,0:T(8,128)(2,1)} %tok_in.1, bf16[128,2048]{1,0:T(8,128)(2,1)} %grad_in.1, bf16[16,2048]{1,0:T(8,128)(2,1)} %bitcast.4, s32[8,128]{1,0:T(8,128)} %bitcast.6, bf16[1,2048,768]{2,1,0:T(8,128)(2,1)} %wg_in.1, bf16[1,2048,768]{2,1,0:T(8,128)(2,1)} %wu_in.1, ...), custom_call_target="tpu_custom_call" | custom-call | tf_op jit(solution)/shard_map/pallas_call | solution.py:326
  113.0 1.3 %copy.11 = f32[128,8]{0,1:T(8,128)} copy(f32[128,8]{0,1:T(8,128)} %bitcast.7) | data formatting | bytes 8192
  114.3 1.3 %copy.12 = f32[128,16]{0,1:T(8,128)} copy(f32[128,16]{0,1:T(8,128)} %bitcast.5) | data formatting | bytes 16384

commit v3 on v2

--- a/solution.py
+++ b/solution.py
@@ -132,8 +132,9 @@
     index_sends = [remote(idx_in, idx.at[q], s_i.at[k], r_i.at[k], plane_dev(k)) for k in range(1, plane)]
     for w in index_sends:
         w.start()
-    pl.when(z == 0)(lambda: own_z("a", UP))
-    pl.when(z == line - 1)(lambda: own_z("a", DOWN))
+    pl.when(z > 0)(lambda: own_z("a", DOWN))
+    pl.when(z < line - 1)(lambda: own_z("a", UP))
+    own_z("c", SIDE)
 
     def relay(kind, s):
         @pl.when(z + s < line)
@@ -192,29 +193,23 @@
             arrived("t", z - s, 1 - y)
             produce(z - s)
 
-    for s in range(1, line):
+    relay("t", 1)
+    for copy in local:
+        copy.wait()
+    for w in weights:
+        w.wait_recv()
+    produce_ring(0)
+    for s in range(2, line):
         relay("t", s)
-        pl.when(z == s)(lambda: own_z("a", UP)) if s < line - 1 else None
-        pl.when(line - 1 - z == s)(lambda: own_z("a", DOWN)) if s < line - 1 else None
-        if s == line - 1:
-            own_z("c", SIDE)
-            own_z("a", SIDE)
-        if s == 1:
-            for copy in local:
-                copy.wait()
-            for w in weights:
-                w.wait_recv()
-        produce_ring(s - 1)
-
-    for s in range(1, line):
-        relay("a", s)
-        if s == 1:
-            produce_ring(line - 1)
-
+    own_z("a", SIDE)
     arrived("c", z, 1 - y)
     for yb in range(2):
         pl.when(z > 0)(lambda yb=yb: piece("c", z, yb, DOWN).start())
         pl.when(z < line - 1)(lambda yb=yb: piece("c", z, yb, UP).start())
+
+    for s in range(1, line):
+        relay("a", s)
+        produce_ring(s)
 
     def reduce_pair(zp):
         @pl.loop(0, 2)

time: 116 us -> 104 us (0.90)
  Pallas kernels: 112 us -> 100 us
    pallas_call x1, Pallas kernels: 112 us -> 100 us  [fused(): pl.pallas_call(functools.partial(layer_kernel, n, dp), out_shape=(jax.Sha...]
where the time goes in v3:
time: 104 us; the launch traced here: 103 us
  Pallas kernels  100 us (96%)
  local copies, waits for them, and re-layouts  2.56 us (2%)
    pallas_call x1, Pallas kernels, fused(): pl.pallas_call(functools.partial(layer_kernel, n, dp), out_shape=(jax.Sha...  100 us
    unnamed x2, local copies, waits for them, and re-layouts  2.56 us

profile of v3, /device:TPU:0, one launch (start us, length us, event | category | flops | bytes accessed | tf_op | source)
XLA Modules:
  0.0 103.5 jit_solution(848484901015747526)
XLA Ops:
  0.6 100.3 %shard_map.86 = (f32[8,128]{1,0:T(8,128)}, f32[16,128]{1,0:T(8,128)}) custom-call(bf16[128,2048]{1,0:T(8,128)(2,1)} %tok_in.1, bf16[128,2048]{1,0:T(8,128)(2,1)} %grad_in.1, bf16[16,2048]{1,0:T(8,128)(2,1)} %bitcast.4, s32[8,128]{1,0:T(8,128)} %bitcast.6, bf16[1,2048,768]{2,1,0:T(8,128)(2,1)} %wg_in.1, bf16[1,2048,768]{2,1,0:T(8,128)(2,1)} %wu_in.1, ...), custom_call_target="tpu_custom_call" | custom-call | tf_op jit(solution)/shard_map/pallas_call | solution.py:321
  100.9 1.3 %copy.11 = f32[128,8]{0,1:T(8,128)} copy(f32[128,8]{0,1:T(8,128)} %bitcast.7) | data formatting | bytes 8192
  102.2 1.3 %copy.12 = f32[128,16]{0,1:T(8,128)} copy(f32[128,16]{0,1:T(8,128)} %bitcast.5) | data formatting | bytes 16384
